TPU v7x, 32 devices: a whole 2x2x4 slice. The times are simulated.
32 devices in a mesh: gx: 4 (over x, core), gy: 8 (over z, y).
Axes of the slice: x: 2, y: 2, z: 4, core: 2. Of those that a mesh axis runs over, the one named last changes fastest.
Arguments:
- tokens: bfloat16 [256, 8192], P('gy', 'gx'), may hold values from -6 to 6
- up_old: bfloat16 [8192, 8192], P(('gx', 'gy')), may hold values from -0.0625 to 0.0625
- down_old: bfloat16 [8192, 8192], P(('gx', 'gy')), may hold values from -0.125 to 0.125
- old_slot: int32 [64], replicated, may hold values from 0 to 63, as said below
- new_owner: int32 [64], replicated, may hold values from 0 to 31, as said below
- hot_rank: int32 [64], replicated, may hold values from 0 to 1, as said below
- route: int32 [256], replicated, may hold values from 0 to 255, each once
Outputs:
- up_new: bfloat16 [8192, 8192], P(('gx', 'gy'))
- down_new: bfloat16 [8192, 8192], P(('gx', 'gy'))
- mixed: bfloat16 [256, 8192], P('gy', 'gx')
Inputs may be any that keep to these rules, and one draw needn't show every extreme that they name: `old_slot`: each slot number appears exactly once. `new_owner`: each device index is the new owner of exactly 2 blocks. `hot_rank`: the blocks of one new owner have distinct ranks.
All inputs are finite; a program needn't handle non-finite values.
Results may differ from a plain program's by a relative error of at most 0.0049.
Values may be sent and summed in bfloat16 or wider, within the bound.
No kernel may reach another device: no remote copies, remote signals or barrier semaphores. Data moves between devices by JAX's collectives and lax.ppermute only.
A program may use at most 128 MiB of HBM per device.

v0:
```python
import jax
import jax.numpy as jnp
from jax import lax
from jax.sharding import PartitionSpec as P

BLOCK = 128


def layer_terms(ordered, up_rows, down_rows):
    pre = lax.dot_general(
        ordered, up_rows, (((1,), (1,)), ((), ())), preferred_element_type=jnp.float32
    )
    hidden = jax.nn.gelu(pre, approximate=False).astype(jnp.bfloat16)
    return jnp.dot(hidden, down_rows, preferred_element_type=jnp.float32)


def relocate(up_old, down_old, old_slot, new_owner, hot_rank):
    held = up_old.shape[0] // BLOCK
    width = up_old.shape[1]
    shaped = (up_old.reshape(held, BLOCK, width), down_old.reshape(held, BLOCK, width))
    spread = (
        lax.all_to_all(shaped[0], ("gx", "gy"), split_axis=1, concat_axis=0, tiled=True),
        lax.all_to_all(shaped[1], ("gx", "gy"), split_axis=1, concat_axis=0, tiled=True),
    )
    total = spread[0].shape[0]
    new_slot = new_owner * held + hot_rank
    source = jnp.zeros((total,), jnp.int32).at[new_slot].set(old_slot)
    picked = (jnp.take(spread[0], source, axis=0), jnp.take(spread[1], source, axis=0))
    landed = (
        lax.all_to_all(picked[0], ("gx", "gy"), split_axis=0, concat_axis=1, tiled=True),
        lax.all_to_all(picked[1], ("gx", "gy"), split_axis=0, concat_axis=1, tiled=True),
    )
    return (landed[0].reshape(held * BLOCK, width), landed[1].reshape(held * BLOCK, width))


def shards(tokens, up_old, down_old, old_slot, new_owner, hot_rank, route):
    feature_rows = lax.all_gather(tokens, "gx", axis=1, tiled=True)
    everyone = lax.all_gather(feature_rows, "gy", axis=0, tiled=True)
    ordered = jnp.take(everyone, route, axis=0)
    partial_out = layer_terms(ordered, up_old, down_old)
    up_new, down_new = relocate(up_old, down_old, old_slot, new_owner, hot_rank)
    by_columns = lax.psum_scatter(partial_out, "gx", scatter_dimension=1, tiled=True)
    summed = lax.psum_scatter(by_columns, "gy", scatter_dimension=0, tiled=True)
    return (up_new, down_new, summed.astype(jnp.bfloat16))


def solution(mesh):
    in_specs = (P("gy", "gx"), P(("gx", "gy"), None), P(("gx", "gy"), None), P(), P(), P(), P())
    out_specs = (P(("gx", "gy"), None), P(("gx", "gy"), None), P("gy", "gx"))
    return jax.shard_map(shards, mesh=mesh, in_specs=in_specs, out_specs=out_specs, check_vma=False)
```

profile of v0, /device:TPU:0, one launch (start us, length us, event | category | flops | bytes accessed | tf_op | source)
XLA Modules:
  0.0 539.0 jit_solution(7738522427065044836)
XLA Ops:
  7.2 8.6 %copy.13 = bf16[2,128,8192]{2,0,1:T(2,128)(2,1)} copy(bf16[2,128,8192]{2,1,0:T(8,128)(2,1)} %bitcast.20) | data formatting | bytes 8388608 | tf_op jit(solution)/shard_map/reshape | solution.py:20
  15.7 0.0 copy-start
  15.7 7.5 %all-to-all-start.2 = ((bf16[2,128,8192]{2,0,1:T(2,128)(2,1)}), bf16[2,128,8192]{2,0,1:T(2,128)(2,1)}, u32[]{:S(2)}, u32[]{:S(2)}) async-start(bf16[2,128,8192]{2,0,1:T(2,128)(2,1)} %copy.13), calls=%async_computation.2 | async-start | bytes 8388608 | tf_op jit(solution)/shard_map/all_to_all | solution.py:23
  23.2 0.0 all-gather.2.cloned.1.call-start
  23.2 0.0 copy-done
  23.3 29.0 %all_gather.6 = bf16[32,8192]{1,0:T(8,128)(2,1)} all-gather(bf16[32,2048]{1,0:T(8,128)(2,1)S(1)} %copy-done), channel_id=1, replica_groups=mesh['gx'=4,'gy'=8] {'gx'}, dimensions={1}, use_global_device_ids=true | all-gather | bytes 655360 | tf_op jit(solution)/shard_map/all_gather | solution.py:37
  52.2 0.0 all-gather.2.cloned.1.call-update
  52.3 8.6 %copy.10 = bf16[2,128,8192]{2,0,1:T(2,128)(2,1)} copy(bf16[2,128,8192]{2,1,0:T(8,128)(2,1)} %bitcast.19) | data formatting | bytes 8388608 | tf_op jit(solution)/shard_map/reshape | solution.py:20
  60.8 0.0 copy-start.1
  60.8 100.0 %all-to-all-done.2 = bf16[2,128,8192]{2,0,1:T(2,128)(2,1)} async-done(((bf16[2,128,8192]{2,0,1:T(2,128)(2,1)}), bf16[2,128,8192]{2,0,1:T(2,128)(2,1)}, u32[]{:S(2)}, u32[]{:S(2)}) %all-to-all-start.2) | async-done | bytes 4194336 | tf_op jit(solution)/shard_map/all_to_all | solution.py:23
  160.9 4.8 all-to-all-start
  165.7 0.5 reduce-scatter.3.cloned.1.call-start
  166.2 0.0 copy-done.1
  166.3 8.4 %all-gather.2.cloned.1.call-done = bf16[256,8192]{1,0:T(8,128)(2,1)} async-done(((bf16[32,8192]{1,0:T(8,128)(2,1)}), bf16[256,8192]{1,0:T(8,128)(2,1)}) %all-gather.2.cloned.1.call-update) | async-done | bytes 4194320 | tf_op jit(solution)/shard_map/all_gather | solution.py:38
  174.7 11.7 %gather_fusion = bf16[256,8192]{1,0:T(8,128)(2,1)} fusion(bf16[256,8192]{1,0:T(8,128)(2,1)} %all-gather.2.cloned.1.call-done, s32[1024]{0:T(1024)S(1)} %pad_clamp_fusion), kind=kCustom, calls=%fused_computation.2 | custom fusion | bytes 8389632 | tf_op jit(solution)/shard_map/jit(_take)/gather | solution.py:39
  186.4 13.0 %fusion.17 = f32[256,8192]{1,0:T(8,128)} fusion(bf16[256,8192]{1,0:T(8,128)(2,1)} %param.11, bf16[256,8192]{1,0:T(8,128)(2,1)} %param.10, bf16[256,8192]{1,0:T(8,128)(2,1)} %gather_fusion, pred[256]{0:T(512)(128)(4,1)S(1)} %compare_and_fusion.1), kind=kOutput, calls=%fused_computation.29 | convolution fusion | flops 2153840640 | bytes 20971776 | tf_op jit(solution)/shard_map/dot_general | solution.py:14
  199.4 0.0 copy-start.2
  199.4 0.0 copy-start.3
  199.4 0.0 reduce-scatter.3.cloned.1.call-update
  199.4 0.6 copy-done.2
  200.0 0.0 copy-done.3
  200.1 1.1 scatter_custom_fusion
  201.2 8.8 %copy.14 = bf16[32,2,4,8192]{3,2,1,0:T(4,128)(2,1)} copy(bf16[32,2,4,8192]{3,1,2,0:T(2,128)(2,1)} %bitcast.8) | data formatting | bytes 8388608 | tf_op jit(solution)/shard_map/all_to_all | solution.py:23
  210.0 51.5 %all-to-all-done = bf16[2,128,8192]{2,0,1:T(2,128)(2,1)} async-done(((bf16[2,128,8192]{2,0,1:T(2,128)(2,1)}), bf16[2,128,8192]{2,0,1:T(2,128)(2,1)}, u32[]{:S(2)}, u32[]{:S(2)}) %all-to-all-start) | async-done | bytes 4194336 | tf_op jit(solution)/shard_map/all_to_all | solution.py:22
  261.5 8.1 %copy.11 = bf16[32,2,4,8192]{3,2,1,0:T(4,128)(2,1)} copy(bf16[32,2,4,8192]{3,1,2,0:T(2,128)(2,1)} %bitcast.2) | data formatting | bytes 8388608 | tf_op jit(solution)/shard_map/all_to_all | solution.py:22
  269.6 8.8 %gather_fusion.2 = bf16[64,4,8192]{2,1,0:T(4,128)(2,1)} fusion(bf16[64,4,8192]{2,1,0:T(4,128)(2,1)} %bitcast.22, s32[1024]{0:T(1024)S(1)} %pad_clamp_fusion.1), kind=kCustom, calls=%fused_computation.1.clone | custom fusion | bytes 8388864 | tf_op jit(solution)/shard_map/jit(_take)/gather | solution.py:28
  278.4 8.5 %gather_fusion.1 = bf16[64,4,8192]{2,1,0:T(4,128)(2,1)} fusion(bf16[64,4,8192]{2,1,0:T(4,128)(2,1)} %bitcast.23, s32[1024]{0:T(1024)S(1)} %pad_clamp_fusion.1), kind=kCustom, calls=%fused_computation.clone | custom fusion | bytes 8388864 | tf_op jit(solution)/shard_map/jit(_take)/gather | solution.py:28
  286.9 7.6 %broadcast_select_fusion = (bf16[64,4,8192]{2,1,0:T(4,128)(2,1)S(1)}, bf16[64,4,8192]{2,1,0:T(4,128)(2,1)}) fusion(bf16[64,4,8192]{2,1,0:T(4,128)(2,1)} %gather_fusion.2, pred[64]{0:T(512)(128)(4,1)S(1)} %compare_and_fusion, bf16[64,4,8192]{2,1,0:T(4,128)(2,1)} %gather_fusion.1), kind=kLoop, calls=%fused_computation.6 | loop fusion | flops 4194304 | bytes 16777280 | tf_op jit(solution)/shard_map/jit(_take)/select_n | solution.py:28
  294.6 97.3 %all_to_all.66 = bf16[64,4,8192]{2,1,0:T(4,128)(2,1)} all-to-all(bf16[64,4,8192]{2,1,0:T(4,128)(2,1)S(1)} %get-tuple-element.4), channel_id=1, replica_groups=mesh['gx'=4,'gy'=8] {'gx','gy'}, dimensions={0} | all-to-all | bytes 8388608 | tf_op jit(solution)/shard_map/all_to_all | solution.py:31
  391.9 3.6 all-to-all-start.1
  395.5 0.0 reduce-scatter.5.cloned.1.call-start
  395.5 0.0 reduce-scatter.3.cloned.1.call-done
  395.6 0.7 reduce-scatter.5.cloned.1.call-update
  396.2 7.3 %copy.15 = bf16[2,32,4,8192]{3,2,1,0:T(4,128)(2,1)} copy(bf16[2,32,4,8192]{3,2,0,1:T(4,128)(2,1)} %bitcast.21) | data formatting | bytes 8388608 | tf_op jit(solution)/shard_map/all_to_all | solution.py:31
  403.5 6.9 %reshape.33 = bf16[256,8192]{1,0:T(8,128)(2,1)} reshape(bf16[2,32,4,8192]{3,2,1,0:T(4,128)(2,1)} %copy.15) | data formatting | bytes 8388608 | tf_op jit(solution)/shard_map/reshape | solution.py:33
  410.3 106.2 %all-to-all-done.1 = bf16[64,4,8192]{2,1,0:T(4,128)(2,1)} async-done(((bf16[64,4,8192]{2,1,0:T(4,128)(2,1)}), bf16[64,4,8192]{2,1,0:T(4,128)(2,1)}, u32[]{:S(2)}, u32[]{:S(2)}) %all-to-all-start.1) | async-done | bytes 4194336 | tf_op jit(solution)/shard_map/all_to_all | solution.py:30
  516.5 7.2 %copy.12 = bf16[2,32,4,8192]{3,2,1,0:T(4,128)(2,1)} copy(bf16[2,32,4,8192]{3,2,0,1:T(4,128)(2,1)} %bitcast.5) | data formatting | bytes 8388608 | tf_op jit(solution)/shard_map/all_to_all | solution.py:30
  523.8 6.9 %reshape.31 = bf16[256,8192]{1,0:T(8,128)(2,1)} reshape(bf16[2,32,4,8192]{3,2,1,0:T(4,128)(2,1)} %copy.12) | data formatting | bytes 8388608 | tf_op jit(solution)/shard_map/reshape | solution.py:33
  530.7 0.0 reduce-scatter.5.cloned.1.call-done
  530.7 1.6 convert_element_type.7
  (7 shorter events, 0.0 us)
Async XLA Ops:
  15.7 7.5 %copy-start = (bf16[32,2048]{1,0:T(8,128)(2,1)S(1)}, bf16[32,2048]{1,0:T(8,128)(2,1)}, u32[]{:S(2)}) copy-start(bf16[32,2048]{1,0:T(8,128)(2,1)} %param.9) | copy-start | bytes 393220
  15.7 145.1 %all-to-all-start.2 = ((bf16[2,128,8192]{2,0,1:T(2,128)(2,1)}), bf16[2,128,8192]{2,0,1:T(2,128)(2,1)}, u32[]{:S(2)}, u32[]{:S(2)}) async-start(bf16[2,128,8192]{2,0,1:T(2,128)(2,1)} %copy.13), calls=%async_computation.2 | async-start | bytes 8388608 | tf_op jit(solution)/shard_map/all_to_all | solution.py:23
  23.2 151.5 %all-gather.2.cloned.1.call-start = ((), (), s32[]{:S(2)}) async-start(), calls=%async_computation.6 | async-start | bytes 4718592 | tf_op jit(solution)/shard_map/all_gather | solution.py:38
  60.8 105.4 %copy-start.1 = (s32[256]{0:T(256)S(1)}, s32[256]{0:T(256)}, u32[]{:S(2)}) copy-start(s32[256]{0:T(256)} %param.15) | copy-start | bytes 3076
  160.9 100.6 %all-to-all-start = ((bf16[2,128,8192]{2,0,1:T(2,128)(2,1)}), bf16[2,128,8192]{2,0,1:T(2,128)(2,1)}, u32[]{:S(2)}, u32[]{:S(2)}) async-start(bf16[2,128,8192]{2,0,1:T(2,128)(2,1)} %copy.10), calls=%async_computation | async-start | bytes 8388608 | tf_op jit(solution)/shard_map/all_to_all | solution.py:22
  165.7 229.8 %reduce-scatter.3.cloned.1.call-start = ((), (), s32[]{:S(2)}) async-start(), calls=%async_computation.7 | async-start | bytes 10485760 | tf_op jit(solution)/shard_map/reduce_scatter | solution.py:42
  199.4 0.7 copy-start.2
  199.4 0.7 copy-start.3
  391.9 124.7 %all-to-all-start.1 = ((bf16[64,4,8192]{2,1,0:T(4,128)(2,1)}), bf16[64,4,8192]{2,1,0:T(4,128)(2,1)}, u32[]{:S(2)}, u32[]{:S(2)}) async-start(bf16[64,4,8192]{2,1,0:T(4,128)(2,1)} %get-tuple-element.5), calls=%async_computation.1 | async-start | bytes 8388608 | tf_op jit(solution)/shard_map/all_to_all | solution.py:30
  395.5 135.2 %reduce-scatter.5.cloned.1.call-start = ((), (), s32[]{:S(2)}) async-start(), calls=%async_computation.8 | async-start | bytes 2359296 | tf_op jit(solution)/shard_map/reduce_scatter | solution.py:43
Sparse Core Ops, SparseCore 0:
  52.4 122.2 all-gather.1
  199.5 77.7 reduce-scatter.2
  399.8 116.0 reduce-scatter.4
where the time goes:
time: 547 us; the launch traced here: 539 us
  waiting for transfers between devices  267 us (49%)
  blocking collectives  126 us (23%)
  local copies, waits for them, and re-layouts  93.1 us (17%)
  starting transfers between devices  16.5 us (3%)
  between operations  14.1 us (3%)
  matrix products  13 us (2%)
  other arithmetic  9.29 us (2%)
    all_to_all x1, waiting for transfers between devices, relocate(): lax.all_to_all(picked[0], ('gx', 'gy'), split_axis=0, concat_axis=1, tile...  106 us
    all_to_all x1, waiting for transfers between devices, relocate(): lax.all_to_all(shaped[1], ('gx', 'gy'), split_axis=1, concat_axis=0, tile...  100 us
    all_to_all x1, blocking collectives, relocate(): lax.all_to_all(picked[1], ('gx', 'gy'), split_axis=0, concat_axis=1, tile...  97.3 us
    all_to_all x1, waiting for transfers between devices, relocate(): lax.all_to_all(shaped[0], ('gx', 'gy'), split_axis=1, concat_axis=0, tile...  51.5 us
    all_gather x1, blocking collectives, shards(): feature_rows = lax.all_gather(tokens, 'gx', axis=1, tiled=True)  29 us
    dot_general x1, matrix products, layer_terms(): return jnp.dot(hidden, down_rows, preferred_element_type=jnp.float32)  13 us
    gather x1, local copies, waits for them, and re-layouts, shards(): ordered = jnp.take(everyone, route, axis=0)  11.7 us
  transfers between devices with their start and end apart: 6, of which 4 were waited for; matrix products, arithmetic and copies ran while one was open for 19% of the time, Pallas kernels for 0%

commit v1 on v0

--- a/solution.py
+++ b/solution.py
@@ -35,7 +35,10 @@
 
 def shards(tokens, up_old, down_old, old_slot, new_owner, hot_rank, route):
     feature_rows = lax.all_gather(tokens, "gx", axis=1, tiled=True)
-    everyone = lax.all_gather(feature_rows, "gy", axis=0, tiled=True)
+    size = lax.axis_size("gy")
+    parts = jnp.stack([feature_rows for _ in range(size)])
+    parts = lax.all_to_all(parts, "gy", split_axis=0, concat_axis=0)
+    everyone = jnp.concatenate(parts, axis=0)
     ordered = jnp.take(everyone, route, axis=0)
     partial_out = layer_terms(ordered, up_old, down_old)
     up_new, down_new = relocate(up_old, down_old, old_slot, new_owner, hot_rank)

time: 547 us -> 603 us (1.10)
  waiting for transfers between devices: 267 us -> 339 us
  blocking collectives: 126 us -> 106 us
    all_to_all x0 -> x1, waiting for transfers between devices: none -> 85.2 us  [shards(): parts = lax.all_to_all(parts, 'gy', split_axis=0, concat_axis=0)]
    all_gather x1, blocking collectives: 29 us -> 8.86 us  [shards(): feature_rows = lax.all_gather(tokens, 'gx', axis=1, tiled=True)]
    all_to_all x1, waiting for transfers between devices: 100 us -> 87.2 us  [relocate(): lax.all_to_all(shaped[1], ('gx', 'gy'), split_axis=1, concat_axis=0, tile...]
    all_to_all x1, waiting for transfers between devices: 51.5 us -> 60.1 us  [relocate(): lax.all_to_all(shaped[0], ('gx', 'gy'), split_axis=1, concat_axis=0, tile...]
    all_gather x1 -> x0, waiting for transfers between devices: 8.39 us -> none  [shards(): everyone = lax.all_gather(feature_rows, 'gy', axis=0, tiled=True)]
where the time goes in v1:
time: 603 us; the launch traced here: 595 us
  waiting for transfers between devices  339 us (56%)
  blocking collectives  106 us (18%)
  local copies, waits for them, and re-layouts  95.4 us (16%)
  starting transfers between devices  17.1 us (3%)
  between operations  14.4 us (2%)
  matrix products  13 us (2%)
  other arithmetic  9.29 us (2%)
    all_to_all x1, waiting for transfers between devices, relocate(): lax.all_to_all(picked[0], ('gx', 'gy'), split_axis=0, concat_axis=1, tile...  106 us
    all_to_all x1, blocking collectives, relocate(): lax.all_to_all(picked[1], ('gx', 'gy'), split_axis=0, concat_axis=1, tile...  97.3 us
    all_to_all x1, waiting for transfers between devices, relocate(): lax.all_to_all(shaped[1], ('gx', 'gy'), split_axis=1, concat_axis=0, tile...  87.2 us
    all_to_all x1, waiting for transfers between devices, shards(): parts = lax.all_to_all(parts, 'gy', split_axis=0, concat_axis=0)  85.2 us
    all_to_all x1, waiting for transfers between devices, relocate(): lax.all_to_all(shaped[0], ('gx', 'gy'), split_axis=1, concat_axis=0, tile...  60.1 us
    dot_general x1, matrix products, layer_terms(): return jnp.dot(hidden, down_rows, preferred_element_type=jnp.float32)  13 us
  transfers between devices with their start and end apart: 6, of which 4 were waited for; matrix products, arithmetic and copies ran while one was open for 19% of the time, Pallas kernels for 0%

profile of v1, /device:TPU:0, one launch (start us, length us, event | category | flops | bytes accessed | tf_op | source)
XLA Modules:
  0.0 594.8 jit_solution(5559120070166465609)
XLA Ops:
  7.2 8.9 %all_gather.3 = bf16[32,8192]{1,0:T(8,128)(2,1)S(1)} all-gather(bf16[32,2048]{1,0:T(8,128)(2,1)} %param.9), channel_id=1, replica_groups=mesh['gx'=4,'gy'=8] {'gx'}, dimensions={1}, use_global_device_ids=true | all-gather | bytes 655360 | tf_op jit(solution)/shard_map/all_gather | solution.py:37
  16.0 2.5 stack.2
  18.5 5.8 all-to-all-start.4
  24.4 8.6 %copy.13 = bf16[2,128,8192]{2,0,1:T(2,128)(2,1)} copy(bf16[2,128,8192]{2,1,0:T(8,128)(2,1)} %bitcast.21) | data formatting | bytes 8388608 | tf_op jit(solution)/shard_map/reshape | solution.py:20
  32.9 85.2 %all-to-all-done.4 = bf16[8,32,8192]{2,1,0:T(8,128)(2,1)} async-done(((bf16[8,32,8192]{2,1,0:T(8,128)(2,1)}), bf16[8,32,8192]{2,1,0:T(8,128)(2,1)}, u32[]{:S(2)}, u32[]{:S(2)}) %all-to-all-start.4) | async-done | bytes 4194336 | tf_op jit(solution)/shard_map/all_to_all | solution.py:40
  118.2 3.6 all-to-all-start.2
  121.8 8.6 %copy.10 = bf16[2,128,8192]{2,0,1:T(2,128)(2,1)} copy(bf16[2,128,8192]{2,1,0:T(8,128)(2,1)} %bitcast.20) | data formatting | bytes 8388608 | tf_op jit(solution)/shard_map/reshape | solution.py:20
  130.3 0.0 copy-start
  130.3 87.2 %all-to-all-done.2 = bf16[2,128,8192]{2,0,1:T(2,128)(2,1)} async-done(((bf16[2,128,8192]{2,0,1:T(2,128)(2,1)}), bf16[2,128,8192]{2,0,1:T(2,128)(2,1)}, u32[]{:S(2)}, u32[]{:S(2)}) %all-to-all-start.2) | async-done | bytes 4194336 | tf_op jit(solution)/shard_map/all_to_all | solution.py:23
  217.5 3.6 all-to-all-start
  221.1 0.5 reduce-scatter.3.cloned.1.call-start
  221.6 0.0 copy-done
  221.7 11.7 %gather_fusion = bf16[256,8192]{1,0:T(8,128)(2,1)} fusion(bf16[256,8192]{1,0:T(8,128)(2,1)} %bitcast.12, s32[1024]{0:T(1024)S(1)} %pad_clamp_fusion), kind=kCustom, calls=%fused_computation.2 | custom fusion | bytes 8389632 | tf_op jit(solution)/shard_map/jit(_take)/gather | solution.py:42
  233.4 13.0 %fusion.17 = f32[256,8192]{1,0:T(8,128)} fusion(bf16[256,8192]{1,0:T(8,128)(2,1)} %param.11, bf16[256,8192]{1,0:T(8,128)(2,1)} %param.10, bf16[256,8192]{1,0:T(8,128)(2,1)} %gather_fusion, pred[256]{0:T(512)(128)(4,1)S(1)} %compare_and_fusion.1), kind=kOutput, calls=%fused_computation.29 | convolution fusion | flops 2153840640 | bytes 20971776 | tf_op jit(solution)/shard_map/dot_general | solution.py:14
  246.4 0.0 copy-start.1
  246.4 0.0 copy-start.2
  246.4 0.0 reduce-scatter.3.cloned.1.call-update
  246.4 0.6 copy-done.1
  247.1 0.0 copy-done.2
  247.1 1.1 scatter_custom_fusion
  248.2 8.7 %copy.14 = bf16[32,2,4,8192]{3,2,1,0:T(4,128)(2,1)} copy(bf16[32,2,4,8192]{3,1,2,0:T(2,128)(2,1)} %bitcast.8) | data formatting | bytes 8388608 | tf_op jit(solution)/shard_map/all_to_all | solution.py:23
  256.8 60.1 %all-to-all-done = bf16[2,128,8192]{2,0,1:T(2,128)(2,1)} async-done(((bf16[2,128,8192]{2,0,1:T(2,128)(2,1)}), bf16[2,128,8192]{2,0,1:T(2,128)(2,1)}, u32[]{:S(2)}, u32[]{:S(2)}) %all-to-all-start) | async-done | bytes 4194336 | tf_op jit(solution)/shard_map/all_to_all | solution.py:22
  316.9 8.1 %copy.11 = bf16[32,2,4,8192]{3,2,1,0:T(4,128)(2,1)} copy(bf16[32,2,4,8192]{3,1,2,0:T(2,128)(2,1)} %bitcast.2) | data formatting | bytes 8388608 | tf_op jit(solution)/shard_map/all_to_all | solution.py:22
  325.1 8.8 %gather_fusion.2 = bf16[64,4,8192]{2,1,0:T(4,128)(2,1)} fusion(bf16[64,4,8192]{2,1,0:T(4,128)(2,1)} %bitcast.23, s32[1024]{0:T(1024)S(1)} %pad_clamp_fusion.1), kind=kCustom, calls=%fused_computation.1.clone | custom fusion | bytes 8388864 | tf_op jit(solution)/shard_map/jit(_take)/gather | solution.py:28
  333.8 8.5 %gather_fusion.1 = bf16[64,4,8192]{2,1,0:T(4,128)(2,1)} fusion(bf16[64,4,8192]{2,1,0:T(4,128)(2,1)} %bitcast.24, s32[1024]{0:T(1024)S(1)} %pad_clamp_fusion.1), kind=kCustom, calls=%fused_computation.clone | custom fusion | bytes 8388864 | tf_op jit(solution)/shard_map/jit(_take)/gather | solution.py:28
  342.4 7.6 %broadcast_select_fusion = (bf16[64,4,8192]{2,1,0:T(4,128)(2,1)S(1)}, bf16[64,4,8192]{2,1,0:T(4,128)(2,1)}) fusion(bf16[64,4,8192]{2,1,0:T(4,128)(2,1)} %gather_fusion.2, pred[64]{0:T(512)(128)(4,1)S(1)} %compare_and_fusion, bf16[64,4,8192]{2,1,0:T(4,128)(2,1)} %gather_fusion.1), kind=kLoop, calls=%fused_computation.6 | loop fusion | flops 4194304 | bytes 16777280 | tf_op jit(solution)/shard_map/jit(_take)/select_n | solution.py:28
  350.0 97.3 %all_to_all.71 = bf16[64,4,8192]{2,1,0:T(4,128)(2,1)} all-to-all(bf16[64,4,8192]{2,1,0:T(4,128)(2,1)S(1)} %get-tuple-element.4), channel_id=1, replica_groups=mesh['gx'=4,'gy'=8] {'gx','gy'}, dimensions={0} | all-to-all | bytes 8388608 | tf_op jit(solution)/shard_map/all_to_all | solution.py:31
  447.3 3.6 all-to-all-start.1
  450.9 0.0 reduce-scatter.5.cloned.1.call-start
  451.0 0.0 reduce-scatter.3.cloned.1.call-done
  451.0 0.7 reduce-scatter.5.cloned.1.call-update
  451.7 7.2 %copy.15 = bf16[2,32,4,8192]{3,2,1,0:T(4,128)(2,1)} copy(bf16[2,32,4,8192]{3,2,0,1:T(4,128)(2,1)} %bitcast.22) | data formatting | bytes 8388608 | tf_op jit(solution)/shard_map/all_to_all | solution.py:31
  458.9 6.9 %reshape.38 = bf16[256,8192]{1,0:T(8,128)(2,1)} reshape(bf16[2,32,4,8192]{3,2,1,0:T(4,128)(2,1)} %copy.15) | data formatting | bytes 8388608 | tf_op jit(solution)/shard_map/reshape | solution.py:33
  465.8 106.2 %all-to-all-done.1 = bf16[64,4,8192]{2,1,0:T(4,128)(2,1)} async-done(((bf16[64,4,8192]{2,1,0:T(4,128)(2,1)}), bf16[64,4,8192]{2,1,0:T(4,128)(2,1)}, u32[]{:S(2)}, u32[]{:S(2)}) %all-to-all-start.1) | async-done | bytes 4194336 | tf_op jit(solution)/shard_map/all_to_all | solution.py:30
  572.0 7.2 %copy.12 = bf16[2,32,4,8192]{3,2,1,0:T(4,128)(2,1)} copy(bf16[2,32,4,8192]{3,2,0,1:T(4,128)(2,1)} %bitcast.5) | data formatting | bytes 8388608 | tf_op jit(solution)/shard_map/all_to_all | solution.py:30
  579.2 6.9 %reshape.36 = bf16[256,8192]{1,0:T(8,128)(2,1)} reshape(bf16[2,32,4,8192]{3,2,1,0:T(4,128)(2,1)} %copy.12) | data formatting | bytes 8388608 | tf_op jit(solution)/shard_map/reshape | solution.py:33
  586.1 0.0 reduce-scatter.5.cloned.1.call-done
  586.1 1.6 convert_element_type.7
  (7 shorter events, 0.0 us)
Async XLA Ops:
  18.5 99.6 %all-to-all-start.4 = ((bf16[8,32,8192]{2,1,0:T(8,128)(2,1)}), bf16[8,32,8192]{2,1,0:T(8,128)(2,1)}, u32[]{:S(2)}, u32[]{:S(2)}) async-start(bf16[8,32,8192]{2,1,0:T(8,128)(2,1)} %stack.2), calls=%async_computation.4 | async-start | bytes 8388608 | tf_op jit(solution)/shard_map/all_to_all | solution.py:40
  118.2 99.4 %all-to-all-start.2 = ((bf16[2,128,8192]{2,0,1:T(2,128)(2,1)}), bf16[2,128,8192]{2,0,1:T(2,128)(2,1)}, u32[]{:S(2)}, u32[]{:S(2)}) async-start(bf16[2,128,8192]{2,0,1:T(2,128)(2,1)} %copy.13), calls=%async_computation.2 | async-start | bytes 8388608 | tf_op jit(solution)/shard_map/all_to_all | solution.py:23
  130.3 91.3 %copy-start = (s32[256]{0:T(256)S(1)}, s32[256]{0:T(256)}, u32[]{:S(2)}) copy-start(s32[256]{0:T(256)} %param.15) | copy-start | bytes 3076
  217.5 99.4 %all-to-all-start = ((bf16[2,128,8192]{2,0,1:T(2,128)(2,1)}), bf16[2,128,8192]{2,0,1:T(2,128)(2,1)}, u32[]{:S(2)}, u32[]{:S(2)}) async-start(bf16[2,128,8192]{2,0,1:T(2,128)(2,1)} %copy.10), calls=%async_computation | async-start | bytes 8388608 | tf_op jit(solution)/shard_map/all_to_all | solution.py:22
  221.1 229.9 %reduce-scatter.3.cloned.1.call-start = ((), (), s32[]{:S(2)}) async-start(), calls=%async_computation.7 | async-start | bytes 10485760 | tf_op jit(solution)/shard_map/reduce_scatter | solution.py:45
  246.4 0.7 copy-start.1
  246.4 0.7 copy-start.2
  447.3 124.7 %all-to-all-start.1 = ((bf16[64,4,8192]{2,1,0:T(4,128)(2,1)}), bf16[64,4,8192]{2,1,0:T(4,128)(2,1)}, u32[]{:S(2)}, u32[]{:S(2)}) async-start(bf16[64,4,8192]{2,1,0:T(4,128)(2,1)} %get-tuple-element.5), calls=%async_computation.1 | async-start | bytes 8388608 | tf_op jit(solution)/shard_map/all_to_all | solution.py:30
  450.9 135.2 %reduce-scatter.5.cloned.1.call-start = ((), (), s32[]{:S(2)}) async-start(), calls=%async_computation.8 | async-start | bytes 2359296 | tf_op jit(solution)/shard_map/reduce_scatter | solution.py:46
Sparse Core Ops, SparseCore 0:
  246.5 83.3 reduce-scatter.2
  455.3 116.0 reduce-scatter.4
